TPU v7x, 32 devices: a whole 2x2x4 slice. The times are simulated.
32 devices in a mesh: gx: 8 (over z, y), gy: 4 (over x, core).
Axes of the slice: x: 2, y: 2, z: 4, core: 2. Of those that a mesh axis runs over, the one named last changes fastest.
Arguments:
- three_index: bfloat16 [8, 4608, 4608], P('gx', 'gy'), as said below
- old_density: bfloat16 [4608, 4608], P('gy'), as said below
- core: float32 [4608, 4608], P('gy', 'gx'), as said below
Outputs:
- purified: bfloat16 [4608, 4608], P('gy', 'gx')
- idempotency: float32 [2], replicated
Inputs may be any that keep to these rules, and one draw needn't show every extreme that they name: Each slab three_index[P] is symmetric in its two basis indices. `old_density`: symmetric. `core`: symmetric.
All inputs are finite; a program needn't handle non-finite values.
Results may differ from a plain program's by a relative error of at most 0.015.
Values may be sent and summed in bfloat16 or wider, within the bound.
A program may use at most 128 MiB of HBM per device.

v0:
```python
import jax
import jax.numpy as jnp
from jax import lax
from jax.sharding import PartitionSpec as P

ITERS = 2


def per_device(three_index, old_density, core):
    aux_dev, rows, width = three_index.shape
    cols = core.shape[1]
    flat = three_index.reshape(aux_dev, rows * width)
    partial_value = jnp.dot(
        flat, old_density.reshape(rows * width), preferred_element_type=jnp.float32
    )
    fitted = lax.psum(partial_value, "gy")
    fitted16 = fitted.astype(jnp.bfloat16)
    coulomb = lax.psum_scatter(
        jnp.einsum("p,prc->cr", fitted16, three_index, preferred_element_type=jnp.float32).astype(
            jnp.bfloat16
        ),
        "gx",
        scatter_dimension=0,
        tiled=True,
    ).astype(jnp.float32)
    fock = core + coulomb.T
    row_start = lax.axis_index("gy") * rows
    col_start = lax.axis_index("gx") * cols
    row_ids = row_start + lax.broadcasted_iota(jnp.int32, (rows, cols), 0)
    col_ids = col_start + lax.broadcasted_iota(jnp.int32, (rows, cols), 1)
    diag_mask = (row_ids == col_ids).astype(jnp.float32)
    local_trace = jnp.sum(fock * diag_mask)
    shift = lax.psum(local_trace, ("gx", "gy")) / width
    shifted = fock - shift * diag_mask
    spread = lax.psum(jnp.sum(shifted * shifted), ("gx", "gy")) / (width * width)
    current = ((shift * diag_mask - fock) / (4.0 * jnp.sqrt(spread + 1e-06))).astype(jnp.bfloat16)
    scale = 1.0 / jnp.sqrt(jnp.float32(width))
    traces = []
    for step in range(ITERS):
        right = lax.all_gather(current, "gy", axis=0, tiled=True)
        row_panel = lax.all_gather(current, "gx", axis=1, tiled=True)
        square_full = jnp.dot(row_panel, right, preferred_element_type=jnp.float32) * scale
        square = square_full.astype(jnp.bfloat16)
        square_block = lax.all_gather(square, "gy", axis=0, tiled=True)
        cube = jnp.dot(row_panel, square_block, preferred_element_type=jnp.float32) * scale
        traces.append(jnp.sum(square_full * diag_mask))
        current = (1.5 * current.astype(jnp.float32) - 2.0 * cube).astype(jnp.bfloat16)
    totals = lax.psum(jnp.stack(traces), ("gx", "gy"))
    idempotency = 16.0 * (0.25 - totals / (width * jnp.sqrt(jnp.float32(width))))
    return (current, idempotency)


def solution(mesh):
    placed = (P("gx", "gy", None), P("gy", None), P("gy", "gx"))
    return jax.shard_map(
        per_device, mesh=mesh, in_specs=placed, out_specs=(P("gy", "gx"), P()), check_vma=False
    )
```

profile of v0, /device:TPU:0, one launch (start us, length us, event | category | flops | bytes accessed | tf_op | source)
XLA Modules:
  0.0 895.6 jit_solution(16187595499375123604)
XLA Ops:
  7.2 0.0 reduce-scatter.2.cloned.1.call-start
  7.2 19.8 %reshape.23 = bf16[5308416]{0:T(1024)(128)(2,1)} reshape(bf16[1,1152,4608]{2,1,0:T(8,128)(2,1)} %param.3) | data formatting | bytes 21233664 | tf_op jit(solution)/shard_map/reshape
  27.0 15.3 %copy.5 = bf16[1,1152,4608]{1,2,0:T(8,128)(2,1)} copy(bf16[1,1152,4608]{2,1,0:T(8,128)(2,1)} %param.3) | data formatting | bytes 21233664 | tf_op args[0]
  42.3 19.8 %reshape.24 = bf16[5308416]{0:T(1024)(128)(2,1)} reshape(bf16[1152,4608]{1,0:T(8,128)(2,1)} %param.4) | data formatting | bytes 21233664 | tf_op jit(solution)/shard_map/reshape | solution.py:14
  62.1 10.9 %fusion = f32[]{:T(128)} fusion(bf16[5308416]{0:T(1024)(128)(2,1)} %reshape.23, bf16[5308416]{0:T(1024)(128)(2,1)} %reshape.24), kind=kLoop, calls=%fused_computation.1 | loop fusion | flops 21233664 | bytes 21233668 | tf_op jit(solution)/shard_map/dot_general | solution.py:13
  72.9 9.0 %psum.28 = bf16[1]{0:T(256)(128)(2,1)} all-reduce(f32[1]{0:T(128)} %bitcast), channel_id=1, replica_groups=mesh['gx'=8,'gy'=4] {'gy'}, use_global_device_ids=true, to_apply=%region_0.0 | all-reduce | flops 1 | bytes 6 | tf_op jit(solution)/shard_map/psum | solution.py:16
  82.6 10.5 %fusion.1 = bf16[4608,1152]{1,0:T(8,128)(2,1)} fusion(bf16[1,1152,4608]{1,2,0:T(8,128)(2,1)} %copy.5, f32[]{:T(128)S(6)} %convert.13), kind=kLoop, calls=%fused_computation.3 | loop fusion | flops 15925248 | bytes 21233668 | tf_op jit(solution)/shard_map/convert_element_type | solution.py:19
  93.1 0.0 all-gather.9.cloned.1.call-start
  93.2 180.8 %reduce-scatter.2.cloned.1.call-done = bf16[576,1152]{1,0:T(8,128)(2,1)} async-done(((bf16[4608,1152]{1,0:T(8,128)(2,1)}), bf16[576,1152]{1,0:T(8,128)(2,1)}) %reduce-scatter.2.cloned.1.call-update) | async-done | bytes 1327120 | tf_op jit(solution)/shard_map/reduce_scatter | solution.py:18
  274.1 2.8 fusion.11
  276.9 39.5 %psum.29 = f32[]{:T(128)} all-reduce(f32[]{:T(128)} %fusion.11), channel_id=1, replica_groups=mesh['gx'=8,'gy'=4] {'gx','gy'}, use_global_device_ids=true, to_apply=%region_3.0 | all-reduce | flops 1 | bytes 8 | tf_op jit(solution)/shard_map/psum | solution.py:33
  317.0 2.9 fusion.10
  319.9 40.2 %psum.30 = f32[]{:T(128)} all-reduce(f32[]{:T(128)} %fusion.10), channel_id=1, replica_groups=mesh['gx'=8,'gy'=4] {'gx','gy'}, use_global_device_ids=true, to_apply=%region_5.0 | all-reduce | flops 1 | bytes 8 | tf_op jit(solution)/shard_map/psum | solution.py:35
  360.8 3.0 fusion.14
  363.8 0.0 all-gather.7.cloned.1.call-start
  363.9 0.7 all-gather.7.cloned.1.call-update
  364.6 40.2 %all-gather.9.cloned.1.call-done = bf16[4608,576]{0,1:T(8,128)(2,1)} async-done(((bf16[1152,576]{0,1:T(8,128)(2,1)}), bf16[4608,576]{0,1:T(8,128)(2,1)}) %all-gather.9.cloned.1.call-update) | async-done | bytes 5308432 | tf_op jit(solution)/shard_map/all_gather | solution.py:40
  404.9 154.9 %all-gather.7.cloned.1.call-done = bf16[1152,4608]{0,1:T(8,128)(2,1)} async-done(((bf16[1152,576]{0,1:T(8,128)(2,1)}), bf16[1152,4608]{0,1:T(8,128)(2,1)}) %all-gather.7.cloned.1.call-update) | async-done | bytes 10616848 | tf_op jit(solution)/shard_map/all_gather | solution.py:41
  559.8 13.3 %fusion.15 = (bf16[1152,576]{0,1:T(8,128)(2,1)}, f32[1152,576]{0,1:T(8,128)}) fusion(bf16[4608,576]{0,1:T(8,128)(2,1)} %all-gather.9.cloned.1.call-done, bf16[1152,4608]{0,1:T(8,128)(2,1)} %all-gather.7.cloned.1.call-done), kind=kOutput, calls=%fused_computation.30 | convolution fusion | flops 6116622336 | bytes 19906560 | tf_op jit(solution)/shard_map/dot_general | solution.py:42
  573.1 0.2 all-gather.15.cloned.1.call-start
  573.4 38.9 %all-gather.11.cloned.1.call-done = bf16[4608,576]{0,1:T(8,128)(2,1)} async-done(((bf16[1152,576]{0,1:T(8,128)(2,1)}), bf16[4608,576]{0,1:T(8,128)(2,1)}) %all-gather.11.cloned.1.call-update) | async-done | bytes 5308432 | tf_op jit(solution)/shard_map/all_gather | solution.py:44
  612.2 12.9 %fusion.7 = bf16[1152,576]{0,1:T(8,128)(2,1)} fusion(bf16[4608,576]{0,1:T(8,128)(2,1)} %all-gather.11.cloned.1.call-done, bf16[1152,4608]{0,1:T(8,128)(2,1)} %all-gather.7.cloned.1.call-done, bf16[1152,576]{0,1:T(8,128)(2,1)S(1)} %copy-done.1), kind=kOutput, calls=%fused_computation.17 | convolution fusion | flops 6118612992 | bytes 18579456 | tf_op jit(solution)/shard_map/dot_general | solution.py:45
  625.1 0.0 all-gather.13.cloned.1.call-start
  625.2 0.5 all-gather.13.cloned.1.call-update
  625.7 0.0 all-gather.17.cloned.1.call-start
  625.7 40.3 %all-gather.15.cloned.1.call-done = bf16[4608,576]{0,1:T(8,128)(2,1)} async-done(((bf16[1152,576]{0,1:T(8,128)(2,1)}), bf16[4608,576]{0,1:T(8,128)(2,1)}) %all-gather.15.cloned.1.call-update) | async-done | bytes 5308432 | tf_op jit(solution)/shard_map/all_gather | solution.py:40
  666.0 154.8 %all-gather.13.cloned.1.call-done = bf16[1152,4608]{0,1:T(8,128)(2,1)} async-done(((bf16[1152,576]{0,1:T(8,128)(2,1)}), bf16[1152,4608]{0,1:T(8,128)(2,1)}) %all-gather.13.cloned.1.call-update) | async-done | bytes 10616848 | tf_op jit(solution)/shard_map/all_gather | solution.py:41
  820.8 14.1 %fusion.12 = (f32[]{:T(128)}, f32[]{:T(128)}, bf16[1152,576]{0,1:T(8,128)(2,1)}) fusion(f32[1152,576]{0,1:T(8,128)} %get-tuple-element.6, s32[1152]{0:T(1024)S(1)} %iota_add_fusion, s32[576]{0:T(1024)S(1)} %iota_add_fusion.1, bf16[4608,576]{0,1:T(8,128)(2,1)} %all-gather.15.cloned.1.call-done, bf16[1152,4608]{0,1:T(8,128)(2,1)} %all-gather.13.cloned.1.call-done), kind=kOutput, calls=%fused_computation.22 | convolution fusion | flops 6119940096 | bytes 19913480 | tf_op jit(solution)/shard_map/dot_general | solution.py:42
  834.9 1.4 pad_maximum_fusion
  836.3 39.1 %psum.31 = f32[2]{0:T(128)S(1)} all-reduce(f32[2]{0:T(128)S(1)} %pad_maximum_fusion), channel_id=1, replica_groups=mesh['gx'=8,'gy'=4] {'gx','gy'}, use_global_device_ids=true, to_apply=%region_8.0 | all-reduce | flops 2 | bytes 16 | tf_op jit(solution)/shard_map/psum | solution.py:48
  875.4 0.5 subtract_multiply_fusion
  875.9 12.9 %fusion.6 = bf16[1152,576]{0,1:T(8,128)(2,1)} fusion(bf16[4608,576]{0,1:T(8,128)(2,1)} %all-gather.17.cloned.1.call-done, bf16[1152,4608]{0,1:T(8,128)(2,1)} %all-gather.13.cloned.1.call-done, bf16[1152,576]{0,1:T(8,128)(2,1)S(1)} %copy-done.2), kind=kOutput, calls=%fused_computation.16 | convolution fusion | flops 6118612992 | bytes 18579456 | tf_op jit(solution)/shard_map/dot_general | solution.py:45
  (15 shorter events, 0.1 us)
Async XLA Ops:
  7.2 266.9 %reduce-scatter.2.cloned.1.call-start = ((), (), s32[]{:S(2)}) async-start(), calls=%async_computation.1 | async-start | bytes 11943936 | tf_op jit(solution)/shard_map/reduce_scatter | solution.py:18
  93.1 181.0 %copy-start = (f32[1152,576]{0,1:T(8,128)S(1)}, f32[1152,576]{0,1:T(8,128)}, u32[]{:S(2)}) copy-start(f32[1152,576]{0,1:T(8,128)} %param.5) | copy-start | bytes 7962628
  93.1 311.7 %all-gather.9.cloned.1.call-start = ((), (), s32[]{:S(2)}) async-start(), calls=%async_computation.3 | async-start | bytes 6635520 | tf_op jit(solution)/shard_map/all_gather | solution.py:40
  363.8 196.0 %all-gather.7.cloned.1.call-start = ((), (), s32[]{:S(2)}) async-start(), calls=%async_computation.2 | async-start | bytes 11943936 | tf_op jit(solution)/shard_map/all_gather | solution.py:41
  364.6 247.7 %copy-start.1 = (bf16[1152,576]{0,1:T(8,128)(2,1)S(1)}, bf16[1152,576]{0,1:T(8,128)(2,1)}, u32[]{:S(2)}) copy-start(bf16[1152,576]{0,1:T(8,128)(2,1)} %fusion.14) | copy-start | bytes 3981316
  364.6 247.6 %all-gather.11.cloned.1.call-start = ((), (), s32[]{:S(2)}) async-start(), calls=%async_computation.4 | async-start | bytes 6635520 | tf_op jit(solution)/shard_map/all_gather | solution.py:44
  573.1 92.9 %all-gather.15.cloned.1.call-start = ((), (), s32[]{:S(2)}) async-start(), calls=%async_computation.6 | async-start | bytes 6635520 | tf_op jit(solution)/shard_map/all_gather | solution.py:40
  625.1 195.7 %all-gather.13.cloned.1.call-start = ((), (), s32[]{:S(2)}) async-start(), calls=%async_computation.5 | async-start | bytes 11943936 | tf_op jit(solution)/shard_map/all_gather | solution.py:41
  625.7 250.2 %all-gather.17.cloned.1.call-start = ((), (), s32[]{:S(2)}) async-start(), calls=%async_computation.7 | async-start | bytes 6635520 | tf_op jit(solution)/shard_map/all_gather | solution.py:44
  820.8 55.1 %copy-start.2 = (bf16[1152,576]{0,1:T(8,128)(2,1)S(1)}, bf16[1152,576]{0,1:T(8,128)(2,1)}, u32[]{:S(2)}) copy-start(bf16[1152,576]{0,1:T(8,128)(2,1)} %fusion.7) | copy-start | bytes 3981316
Sparse Core Ops, SparseCore 0:
  93.3 180.7 reduce-scatter.1
  363.9 40.8 all-gather.8
  407.6 152.1 all-gather.6
  573.3 38.9 all-gather.10
  625.2 40.7 all-gather.14
  668.6 152.1 all-gather.12
  835.0 39.4 all-gather.16
where the time goes:
time: 897 us; the launch traced here: 896 us
  waiting for transfers between devices  611 us (68%)
  blocking collectives  128 us (14%)
  local copies, waits for them, and re-layouts  54.9 us (6%)
  matrix products  53.1 us (6%)
  other arithmetic  32 us (4%)
  between operations  16.2 us (2%)
    all_gather x2, waiting for transfers between devices, per_device(): row_panel = lax.all_gather(current, 'gx', axis=1, tiled=True)  310 us
    reduce_scatter x1, waiting for transfers between devices, per_device(): lax.psum_scatter(jnp.einsum('p,prc->cr', fitted16, three_index, preferred...  181 us
    all_gather x2, waiting for transfers between devices, per_device(): right = lax.all_gather(current, 'gy', axis=0, tiled=True)  80.5 us
    psum x1, blocking collectives, per_device(): lax.psum(jnp.sum(shifted * shifted), ('gx', 'gy')) / (width * width)  40.2 us
    psum x1, blocking collectives, per_device(): shift = lax.psum(local_trace, ('gx', 'gy')) / width  39.5 us
    psum x1, blocking collectives, per_device(): totals = lax.psum(jnp.stack(traces), ('gx', 'gy'))  39.1 us
    all_gather x2, waiting for transfers between devices, per_device(): square_block = lax.all_gather(square, 'gy', axis=0, tiled=True)  38.9 us
    dot_general x2, matrix products, per_device(): jnp.dot(row_panel, right, preferred_element_type=jnp.float32) * scale  27.4 us
  transfers between devices with their start and end apart: 7, of which 6 were waited for; matrix products, arithmetic and copies ran while one was open for 0% of the time, Pallas kernels for 0%

commit v1 on v0

--- a/solution.py
+++ b/solution.py
@@ -38,7 +38,7 @@
     traces = []
     for step in range(ITERS):
         right = lax.all_gather(current, "gy", axis=0, tiled=True)
-        row_panel = lax.all_gather(current, "gx", axis=1, tiled=True)
+        row_panel = jnp.concatenate(lax.all_gather(current, "gx"), axis=1)
         square_full = jnp.dot(row_panel, right, preferred_element_type=jnp.float32) * scale
         square = square_full.astype(jnp.bfloat16)
         square_block = lax.all_gather(square, "gy", axis=0, tiled=True)

time: 897 us -> 895 us (level)
  waiting for transfers between devices: 611 us -> 588 us
  local copies, waits for them, and re-layouts: 54.9 us -> 74 us
    all_gather x0 -> x2, local copies, waits for them, and re-layouts: none -> 19.1 us  [per_device(): row_panel = jnp.concatenate(lax.all_gather(current, 'gx'), axis=1)]
    all_gather x2, waiting for transfers between devices: 80.5 us -> 62.9 us  [per_device(): right = lax.all_gather(current, 'gy', axis=0, tiled=True)]
  transfers between devices with their start and end apart: 7 -> 7, of which waited for: 6 -> 6; matrix products, arithmetic and copies ran while one was open for 0% -> 2% of each run, Pallas kernels for 0% -> 0%
where the time goes in v1:
time: 895 us; the launch traced here: 893 us
  waiting for transfers between devices  588 us (66%)
  blocking collectives  129 us (14%)
  local copies, waits for them, and re-layouts  74 us (8%)
  matrix products  53.2 us (6%)
  other arithmetic  31.9 us (4%)
  between operations  16.2 us (2%)
    all_gather x2, waiting for transfers between devices, per_device(): row_panel = jnp.concatenate(lax.all_gather(current, 'gx'), axis=1)  303 us
    reduce_scatter x1, waiting for transfers between devices, per_device(): lax.psum_scatter(jnp.einsum('p,prc->cr', fitted16, three_index, preferred...  181 us
    all_gather x2, waiting for transfers between devices, per_device(): right = lax.all_gather(current, 'gy', axis=0, tiled=True)  62.9 us
    all_gather x2, waiting for transfers between devices, per_device(): square_block = lax.all_gather(square, 'gy', axis=0, tiled=True)  40.7 us
    psum x1, blocking collectives, per_device(): lax.psum(jnp.sum(shifted * shifted), ('gx', 'gy')) / (width * width)  40.2 us
    psum x1, blocking collectives, per_device(): totals = lax.psum(jnp.stack(traces), ('gx', 'gy'))  40 us
    psum x1, blocking collectives, per_device(): shift = lax.psum(local_trace, ('gx', 'gy')) / width  39.5 us
    dot_general x2, matrix products, per_device(): jnp.dot(row_panel, right, preferred_element_type=jnp.float32) * scale  27.4 us
  transfers between devices with their start and end apart: 7, of which 6 were waited for; matrix products, arithmetic and copies ran while one was open for 2% of the time, Pallas kernels for 0%

profile of v1, /device:TPU:0, one launch (start us, length us, event | category | flops | bytes accessed | tf_op | source)
XLA Modules:
  0.0 892.6 jit_solution(8236411339931251218)
XLA Ops:
  7.2 19.8 %reshape.35 = bf16[5308416]{0:T(1024)(128)(2,1)} reshape(bf16[1,1152,4608]{2,1,0:T(8,128)(2,1)} %param.3) | data formatting | bytes 21233664 | tf_op jit(solution)/shard_map/reshape
  27.0 15.3 %copy.6 = bf16[1,1152,4608]{1,2,0:T(8,128)(2,1)} copy(bf16[1,1152,4608]{2,1,0:T(8,128)(2,1)} %param.3) | data formatting | bytes 21233664 | tf_op args[0]
  42.3 19.8 %reshape.36 = bf16[5308416]{0:T(1024)(128)(2,1)} reshape(bf16[1152,4608]{1,0:T(8,128)(2,1)} %param.4) | data formatting | bytes 21233664 | tf_op jit(solution)/shard_map/reshape | solution.py:14
  62.1 10.9 %fusion = f32[]{:T(128)} fusion(bf16[5308416]{0:T(1024)(128)(2,1)} %reshape.35, bf16[5308416]{0:T(1024)(128)(2,1)} %reshape.36), kind=kLoop, calls=%fused_computation.1 | loop fusion | flops 21233664 | bytes 21233668 | tf_op jit(solution)/shard_map/dot_general | solution.py:13
  72.9 9.0 %psum.28 = bf16[1]{0:T(256)(128)(2,1)} all-reduce(f32[1]{0:T(128)} %bitcast), channel_id=1, replica_groups=mesh['gx'=8,'gy'=4] {'gy'}, use_global_device_ids=true, to_apply=%region_0.0 | all-reduce | flops 1 | bytes 6 | tf_op jit(solution)/shard_map/psum | solution.py:16
  82.6 10.5 %fusion.1 = bf16[4608,1152]{1,0:T(8,128)(2,1)} fusion(bf16[1,1152,4608]{1,2,0:T(8,128)(2,1)} %copy.6, f32[]{:T(128)S(6)} %convert.13), kind=kLoop, calls=%fused_computation.3 | loop fusion | flops 15925248 | bytes 21233668 | tf_op jit(solution)/shard_map/convert_element_type | solution.py:19
  93.1 0.0 all-gather.17.cloned.1.call-start
  93.2 180.8 %reduce-scatter.2.cloned.1.call-done = bf16[576,1152]{1,0:T(8,128)(2,1)} async-done(((bf16[4608,1152]{1,0:T(8,128)(2,1)}), bf16[576,1152]{1,0:T(8,128)(2,1)}) %reduce-scatter.2.cloned.1.call-update) | async-done | bytes 1327120 | tf_op jit(solution)/shard_map/reduce_scatter | solution.py:18
  274.1 2.8 fusion.11
  276.9 39.5 %psum.29 = f32[]{:T(128)} all-reduce(f32[]{:T(128)} %fusion.11), channel_id=1, replica_groups=mesh['gx'=8,'gy'=4] {'gx','gy'}, use_global_device_ids=true, to_apply=%region_3.0 | all-reduce | flops 1 | bytes 8 | tf_op jit(solution)/shard_map/psum | solution.py:33
  317.0 2.9 fusion.10
  319.9 40.2 %psum.30 = f32[]{:T(128)} all-reduce(f32[]{:T(128)} %fusion.10), channel_id=1, replica_groups=mesh['gx'=8,'gy'=4] {'gx','gy'}, use_global_device_ids=true, to_apply=%region_5.0 | all-reduce | flops 1 | bytes 8 | tf_op jit(solution)/shard_map/psum | solution.py:35
  360.8 3.0 fusion.14
  363.8 0.0 all-gather.9.cloned.1.call-start
  363.9 0.7 all-gather.9.cloned.1.call-update
  364.6 151.2 %all-gather.17.cloned.1.call-done = bf16[9216,576]{0,1:T(8,128)(2,1)} async-done(((bf16[1152,576]{0,1:T(8,128)(2,1)}), bf16[9216,576]{0,1:T(8,128)(2,1)}) %all-gather.17.cloned.1.call-update) | async-done | bytes 10616848 | tf_op jit(solution)/shard_map/all_gather | solution.py:41
  515.9 9.6 %copy.17 = bf16[72,8,8,1152]{3,2,0,1:T(8,128)(2,1)} copy(bf16[72,8,8,1152]{3,2,1,0:T(8,128)(2,1)} %bitcast.43) | data formatting | bytes 21233664 | tf_op jit(solution)/shard_map/all_gather | solution.py:41
  525.4 31.6 %all-gather.9.cloned.1.call-done = bf16[4608,576]{0,1:T(8,128)(2,1)} async-done(((bf16[1152,576]{0,1:T(8,128)(2,1)}), bf16[4608,576]{0,1:T(8,128)(2,1)}) %all-gather.9.cloned.1.call-update) | async-done | bytes 5308432 | tf_op jit(solution)/shard_map/all_gather | solution.py:40
  557.0 13.4 %fusion.15 = (bf16[1152,576]{0,1:T(8,128)(2,1)}, f32[1152,576]{0,1:T(8,128)}) fusion(bf16[4608,576]{0,1:T(8,128)(2,1)} %all-gather.9.cloned.1.call-done, bf16[1152,4608]{0,1:T(8,128)(2,1)} %bitcast.41), kind=kOutput, calls=%fused_computation.32 | convolution fusion | flops 6116622336 | bytes 19906560 | tf_op jit(solution)/shard_map/dot_general | solution.py:42
  570.4 0.2 all-gather.19.cloned.1.call-start
  570.6 40.7 %all-gather.11.cloned.1.call-done = bf16[4608,576]{0,1:T(8,128)(2,1)} async-done(((bf16[1152,576]{0,1:T(8,128)(2,1)}), bf16[4608,576]{0,1:T(8,128)(2,1)}) %all-gather.11.cloned.1.call-update) | async-done | bytes 5308432 | tf_op jit(solution)/shard_map/all_gather | solution.py:44
  611.3 12.9 %fusion.7 = bf16[1152,576]{0,1:T(8,128)(2,1)} fusion(bf16[4608,576]{0,1:T(8,128)(2,1)} %all-gather.11.cloned.1.call-done, bf16[1152,4608]{0,1:T(8,128)(2,1)} %bitcast.42, bf16[1152,576]{0,1:T(8,128)(2,1)S(1)} %copy-done.1), kind=kOutput, calls=%fused_computation.19 | convolution fusion | flops 6118612992 | bytes 18579456 | tf_op jit(solution)/shard_map/dot_general | solution.py:45
  624.2 0.0 all-gather.13.cloned.1.call-start
  624.3 0.5 all-gather.13.cloned.1.call-update
  624.8 151.3 %all-gather.19.cloned.1.call-done = bf16[9216,576]{0,1:T(8,128)(2,1)} async-done(((bf16[1152,576]{0,1:T(8,128)(2,1)}), bf16[9216,576]{0,1:T(8,128)(2,1)}) %all-gather.19.cloned.1.call-update) | async-done | bytes 10616848 | tf_op jit(solution)/shard_map/all_gather | solution.py:41
  776.1 9.6 %copy.16 = bf16[72,8,8,1152]{3,2,0,1:T(8,128)(2,1)} copy(bf16[72,8,8,1152]{3,2,1,0:T(8,128)(2,1)} %bitcast.44) | data formatting | bytes 21233664 | tf_op jit(solution)/shard_map/all_gather | solution.py:41
  785.7 31.4 %all-gather.13.cloned.1.call-done = bf16[4608,576]{0,1:T(8,128)(2,1)} async-done(((bf16[1152,576]{0,1:T(8,128)(2,1)}), bf16[4608,576]{0,1:T(8,128)(2,1)}) %all-gather.13.cloned.1.call-update) | async-done | bytes 5308432 | tf_op jit(solution)/shard_map/all_gather | solution.py:40
  817.1 14.0 %fusion.12 = (f32[]{:T(128)}, f32[]{:T(128)}, bf16[1152,576]{0,1:T(8,128)(2,1)}) fusion(f32[1152,576]{0,1:T(8,128)} %get-tuple-element.6, s32[1152]{0:T(1024)S(1)} %iota_add_fusion, s32[576]{0:T(1024)S(1)} %iota_add_fusion.1, bf16[4608,576]{0,1:T(8,128)(2,1)} %all-gather.13.cloned.1.call-done, bf16[1152,4608]{0,1:T(8,128)(2,1)} %bitcast.39), kind=kOutput, calls=%fused_computation.24 | convolution fusion | flops 6119940096 | bytes 19913480 | tf_op jit(solution)/shard_map/dot_general | solution.py:42
  831.1 1.3 pad_maximum_fusion
  832.4 40.0 %psum.31 = f32[2]{0:T(128)S(1)} all-reduce(f32[2]{0:T(128)S(1)} %pad_maximum_fusion), channel_id=1, replica_groups=mesh['gx'=8,'gy'=4] {'gx','gy'}, use_global_device_ids=true, to_apply=%region_8.0 | all-reduce | flops 2 | bytes 16 | tf_op jit(solution)/shard_map/psum | solution.py:48
  872.4 0.5 subtract_multiply_fusion
  872.9 12.9 %fusion.6 = bf16[1152,576]{0,1:T(8,128)(2,1)} fusion(bf16[4608,576]{0,1:T(8,128)(2,1)} %all-gather.15.cloned.1.call-done, bf16[1152,4608]{0,1:T(8,128)(2,1)} %bitcast.40, bf16[1152,576]{0,1:T(8,128)(2,1)S(1)} %copy-done.2), kind=kOutput, calls=%fused_computation.18 | convolution fusion | flops 6118612992 | bytes 18579456 | tf_op jit(solution)/shard_map/dot_general | solution.py:45
  (17 shorter events, 0.2 us)
Async XLA Ops:
  7.2 266.9 %reduce-scatter.2.cloned.1.call-start = ((), (), s32[]{:S(2)}) async-start(), calls=%async_computation.1 | async-start | bytes 11943936 | tf_op jit(solution)/shard_map/reduce_scatter | solution.py:18
  93.1 181.0 %copy-start = (f32[1152,576]{0,1:T(8,128)S(1)}, f32[1152,576]{0,1:T(8,128)}, u32[]{:S(2)}) copy-start(f32[1152,576]{0,1:T(8,128)} %param.5) | copy-start | bytes 7962628
  93.1 422.7 %all-gather.17.cloned.1.call-start = ((), (), s32[]{:S(2)}) async-start(), calls=%async_computation.6 | async-start | bytes 11943936 | tf_op jit(solution)/shard_map/all_gather | solution.py:41
  363.8 193.1 %all-gather.9.cloned.1.call-start = ((), (), s32[]{:S(2)}) async-start(), calls=%async_computation.2 | async-start | bytes 6635520 | tf_op jit(solution)/shard_map/all_gather | solution.py:40
  364.6 246.8 %all-gather.11.cloned.1.call-start = ((), (), s32[]{:S(2)}) async-start(), calls=%async_computation.3 | async-start | bytes 6635520 | tf_op jit(solution)/shard_map/all_gather | solution.py:44
  557.0 54.4 %copy-start.1 = (bf16[1152,576]{0,1:T(8,128)(2,1)S(1)}, bf16[1152,576]{0,1:T(8,128)(2,1)}, u32[]{:S(2)}) copy-start(bf16[1152,576]{0,1:T(8,128)(2,1)} %fusion.14) | copy-start | bytes 3981316
  570.4 205.7 %all-gather.19.cloned.1.call-start = ((), (), s32[]{:S(2)}) async-start(), calls=%async_computation.7 | async-start | bytes 11943936 | tf_op jit(solution)/shard_map/all_gather | solution.py:41
  624.2 192.9 %all-gather.13.cloned.1.call-start = ((), (), s32[]{:S(2)}) async-start(), calls=%async_computation.4 | async-start | bytes 6635520 | tf_op jit(solution)/shard_map/all_gather | solution.py:40
  624.8 248.1 %all-gather.15.cloned.1.call-start = ((), (), s32[]{:S(2)}) async-start(), calls=%async_computation.5 | async-start | bytes 6635520 | tf_op jit(solution)/shard_map/all_gather | solution.py:44
  817.1 55.9 %copy-start.2 = (bf16[1152,576]{0,1:T(8,128)(2,1)S(1)}, bf16[1152,576]{0,1:T(8,128)(2,1)}, u32[]{:S(2)}) copy-start(bf16[1152,576]{0,1:T(8,128)(2,1)} %fusion.7) | copy-start | bytes 3981316
Sparse Core Ops, SparseCore 0:
  93.3 180.7 reduce-scatter.1
  363.9 151.8 all-gather.16
  518.0 38.9 all-gather.8
  570.5 40.7 all-gather.10
  624.3 151.7 all-gather.18
  778.1 38.9 all-gather.12
  831.2 41.4 all-gather.14
